TPU v7x, 512 devices: a whole 4x4x16 slice. The times are simulated.
512 devices in a mesh: dp: 64 (over z, y_lo, core), mp: 8 (over x, y_hi).
Axes of the slice: x: 4, y: 4 (y_hi: 2, y_lo: 2; y = y_hi * 2 + y_lo), z: 16, core: 2. Of those that a mesh axis runs over, the one named last changes fastest.
Arguments:
- picture_tower_vectors: bfloat16 [12288, 1152], P('dp'), may hold values from -6 to 6
- caption_tower_vectors: bfloat16 [12288, 1152], P('dp', 'mp'), may hold values from -6 to 6
- picture_standardize_factor: float32 [1152], replicated, may hold values from 0.1 to 1.9
- picture_entry_matrix: bfloat16 [1152, 4304], P(None, 'mp'), may hold values from -0.1875 to 0.1875
- picture_exit_matrix: bfloat16 [4304, 1152], P('mp'), may hold values from -0.09375 to 0.09375
- caption_mapping_matrix: bfloat16 [1152, 1152], P('mp'), may hold values from -1 to 1
- energy_multiplier: float32 [], replicated, may hold values from 4 to 16
- energy_offset_term: float32 [], replicated, may hold values from -2 to -0.5
Outputs:
- grad_image: float32 [12288, 1152], P('dp', 'mp')
- grad_text: float32 [12288, 1152], P('dp', 'mp')
All inputs are finite; a program needn't handle non-finite values.
Results may differ from a plain program's by a relative error of at most 0.0046.
Values may be sent and summed in bfloat16 or wider, within the bound.
No kernel may reach another device: no remote copies, remote signals or barrier semaphores. Data moves between devices by JAX's collectives and lax.ppermute only.
A program may use at most 64 MiB of HBM per device.

v0:
```python
import jax
import jax.numpy as jnp
from jax import lax
from jax.sharding import Mesh
from jax.sharding import PartitionSpec as P

DP = ("dp_0", "dp_1", "dp_2")


def cut_along(array, dim, peers):
    lengths = array.shape
    parts = array.reshape(*lengths[:dim], peers, lengths[dim] // peers, *lengths[dim + 1 :])
    return jnp.moveaxis(parts, dim, 0)


def summed_on_arrival(array, axis, dim):
    peers = lax.axis_size(axis)
    parts = lax.all_to_all(cut_along(array, dim, peers), axis, 0, 0, tiled=True)
    return jnp.sum(parts.astype(jnp.float32), axis=0)


def in_order(parts, dim):
    lengths = list(parts.shape[1:])
    lengths[dim] *= parts.shape[0]
    return jnp.moveaxis(parts, 0, dim).reshape(lengths)


def stacked_from(array, axes, order):
    parts = array[None]
    for k in order:
        parts = lax.all_gather(parts, axes[k], axis=0, tiled=True)
    block = [lax.axis_size(axes[k]) for k in reversed(order)]
    parts = parts.reshape(*block, *array.shape)
    turned = sorted(range(len(order)), key=lambda place: order[len(order) - 1 - place])
    return parts.transpose(*turned, *range(len(order), parts.ndim)).reshape(-1, *array.shape)


def whole_of(array, axes, order, dim):
    return in_order(stacked_from(array, axes, order), dim)


def sum_at_owner(array, axis, dim):
    parts = cut_along(array, dim, lax.axis_size(axis))
    arrived = lax.all_to_all(parts, axis, split_axis=0, concat_axis=0, tiled=True)
    return arrived.sum(axis=0)


def sent_to_all(array, axis):
    copies = jnp.broadcast_to(array, (lax.axis_size(axis), *array.shape))
    return lax.all_to_all(copies, axis, split_axis=0, concat_axis=0, tiled=True)


def collect(array, axis, dim):
    return in_order(sent_to_all(array, axis), dim)


def of_everyone(array, axis):
    return sent_to_all(array, axis).sum(axis=0)


def together(arrays, axis):
    ends = [0]
    for a in arrays:
        ends.append(ends[-1] + a.size)
    so_far = of_everyone(jnp.concatenate([a.ravel() for a in arrays]), axis)
    return tuple((so_far[b:e].reshape(a.shape) for a, b, e in zip(arrays, ends, ends[1:])))


def gelu_tanh(values):
    return jax.nn.gelu(values, approximate=True)


def norm_back(upstream, unit_rows, inverse):
    unit_float = unit_rows.astype(jnp.float32)
    along = jnp.sum(unit_float * upstream, axis=-1, keepdims=True)
    return inverse * (upstream - unit_float * along)


def per_device(
    picture_tower_vectors,
    caption_tower_vectors,
    picture_standardize_factor,
    picture_entry_matrix,
    picture_exit_matrix,
    caption_mapping_matrix,
    energy_multiplier,
    energy_offset_term,
):
    rows_here = picture_tower_vectors.shape[0]
    width = picture_tower_vectors.shape[1]
    head_count = lax.axis_size("mp")
    head_pos = lax.axis_index("mp")
    cycle_size = lax.axis_size(DP)
    cycle_pos = lax.axis_index(DP)
    share = rows_here // head_count
    cols_here = caption_tower_vectors.shape[1]
    image_float = picture_tower_vectors.astype(jnp.float32)
    mean_row = jnp.mean(image_float, axis=-1, keepdims=True)
    variance = jnp.mean((image_float - mean_row) ** 2, axis=-1, keepdims=True)
    inv_std = lax.rsqrt(variance + 1e-06)
    centred = (image_float - mean_row) * inv_std
    normed = (centred * picture_standardize_factor).astype(jnp.bfloat16)
    preact = jnp.dot(normed, picture_entry_matrix, preferred_element_type=jnp.float32)
    hidden = gelu_tanh(preact).astype(jnp.bfloat16)
    partial_out = jnp.dot(hidden, picture_exit_matrix, preferred_element_type=jnp.float32)
    image_out = image_float + lax.psum(partial_out, "mp")
    inv_image = lax.rsqrt(jnp.sum(image_out * image_out, axis=-1, keepdims=True) + 1e-06)
    unit_image = (image_out * inv_image).astype(jnp.bfloat16)
    text_out = summed_on_arrival(
        jnp.dot(
            caption_tower_vectors, caption_mapping_matrix, preferred_element_type=jnp.float32
        ).astype(jnp.bfloat16),
        "mp",
        0,
    )
    inv_text = lax.rsqrt(jnp.sum(text_out * text_out, axis=-1, keepdims=True) + 1e-06)
    unit_text = (text_out * inv_text).astype(jnp.bfloat16)
    image_ids = cycle_pos * rows_here + jnp.arange(rows_here, dtype=jnp.int32)
    piece = whole_of(unit_text, DP, (1, 0, 2), 0)
    count = piece.shape[0]
    whole_pos = jnp.arange(count, dtype=jnp.int32)
    text_ids = whole_pos // share * rows_here + head_pos * share + whole_pos % share
    cosine_matrix = lax.dot_general(
        piece, unit_image, (((1,), (1,)), ((), ())), preferred_element_type=jnp.float32
    )
    couple_energies = energy_multiplier * cosine_matrix + energy_offset_term
    match_polarity = jnp.where(text_ids[:, None] == image_ids[None, :], 1.0, -1.0).astype(
        jnp.float32
    )
    polarity_scaled_energies = (
        energy_multiplier * -match_polarity * jax.nn.sigmoid(-match_polarity * couple_energies)
    ).astype(jnp.bfloat16)
    image_add = lax.dot_general(
        polarity_scaled_energies,
        piece,
        (((0,), (0,)), ((), ())),
        preferred_element_type=jnp.float32,
    )
    text_add = jnp.dot(polarity_scaled_energies, unit_image, preferred_element_type=jnp.float32)
    image_add, text_add = (image_add, text_add)
    text_store = text_add
    image_dir, text_store = (image_add, text_store)
    returned = lax.all_to_all(
        text_store.astype(jnp.bfloat16), DP, split_axis=0, concat_axis=0, tiled=True
    ).astype(text_store.dtype)
    text_dir = jnp.sum(returned.reshape(cycle_size, share, width), axis=0)
    image_share = sum_at_owner(image_dir, "mp", 0)
    first_row = head_pos * share
    unit_share = lax.dynamic_slice_in_dim(unit_image, first_row, share, 0)
    inv_share = lax.dynamic_slice_in_dim(inv_image, first_row, share, 0)
    grad_share = norm_back(image_share, unit_share, inv_share)
    grad_out = collect(grad_share, "mp", 0)
    grad_out_b = grad_out.astype(jnp.bfloat16)
    grad_hidden = lax.dot_general(
        grad_out_b,
        picture_exit_matrix,
        (((1,), (1,)), ((), ())),
        preferred_element_type=jnp.float32,
    )
    unused, pull_back = jax.vjp(gelu_tanh, preact)
    grad_pre = pull_back(grad_hidden)[0].astype(jnp.bfloat16)
    partial_normed = lax.dot_general(
        grad_pre, picture_entry_matrix, (((1,), (1,)), ((), ())), preferred_element_type=jnp.float32
    )
    grad_normed = sum_at_owner(partial_normed, "mp", 1)
    first_col = head_pos * cols_here
    gain_here = lax.dynamic_slice_in_dim(picture_standardize_factor, first_col, cols_here, 0)
    centred_here = lax.dynamic_slice_in_dim(centred, first_col, cols_here, 1)
    grad_out_here = lax.dynamic_slice_in_dim(grad_out, first_col, cols_here, 1)
    scaled = grad_normed * gain_here
    sum_one, sum_two = together(
        (jnp.sum(scaled, axis=-1), jnp.sum(scaled * centred_here, axis=-1)), "mp"
    )
    mean_one = (sum_one / width)[:, None]
    mean_two = (sum_two / width)[:, None]
    grad_image = grad_out_here + inv_std * (scaled - mean_one - centred_here * mean_two)
    grad_text_out = norm_back(text_dir, unit_text, inv_text).astype(jnp.bfloat16)
    grad_text = lax.dot_general(
        collect(grad_text_out, "mp", 0),
        caption_mapping_matrix,
        (((1,), (1,)), ((), ())),
        preferred_element_type=jnp.float32,
    )
    return (grad_image, grad_text)


def solution(mesh):
    split = Mesh(mesh.devices.reshape(16, 2, 2, mesh.shape["mp"]), ("dp_0", "dp_1", "dp_2", "mp"))
    in_specs = (
        P(DP, None),
        P(DP, "mp"),
        P(),
        P(None, "mp"),
        P("mp", None),
        P("mp", None),
        P(),
        P(),
    )
    out_specs = (P(DP, "mp"), P(DP, "mp"))
    return jax.shard_map(
        per_device, mesh=split, in_specs=in_specs, out_specs=out_specs, check_vma=False
    )
```

profile of v0, /device:TPU:8, one launch (start us, length us, event | category | flops | bytes accessed | tf_op | source)
XLA Modules:
  0.0 417.5 jit_solution(5761427556059178533)
XLA Ops:
  8.1 1.4 convolution_convert_fusion.1
  9.5 16.4 %all_to_all.40 = bf16[8,24,1152]{2,1,0:T(8,128)(2,1)S(1)} all-to-all(bf16[8,24,1152]{2,1,0:T(8,128)(2,1)S(1)} %bitcast.50), channel_id=1, replica_groups=mesh['dp_0'=16,'dp_1'=2,'dp_2'=2,'mp'=8] {'mp'}, dimensions={0} | all-to-all | bytes 884736 | tf_op jit(solution)/shard_map/all_to_all | solution.py:18
  26.2 4.9 %all_gather.9 = bf16[2,24,1152]{2,1,0:T(8,128)(2,1)} all-gather(bf16[1,24,1152]{2,1,0:T(8,128)(2,1)S(1)} %fusion.50), channel_id=1, replica_groups=mesh['dp_0'=16,'dp_1'=2,'dp_2'=2,'mp'=8] {'dp_1'}, dimensions={0}, use_global_device_ids=true | all-gather | bytes 165888 | tf_op jit(solution)/shard_map/all_gather | solution.py:31
  31.7 2.0 fusion.22
  33.7 1.5 fusion.32
  35.2 69.5 %all-gather.3.cloned.1.call-done = bf16[32,24,1152]{2,1,0:T(8,128)(2,1)} async-done(((bf16[2,24,1152]{2,1,0:T(8,128)(2,1)}), bf16[32,24,1152]{2,1,0:T(8,128)(2,1)}) %all-gather.3.cloned.1.call-update) | async-done | bytes 1769488 | tf_op jit(solution)/shard_map/all_gather | solution.py:31
  106.1 33.0 %all-reduce.2.cloned.1.call-done = f32[192,1152]{1,0:T(8,128)} async-done(((f32[192,1152]{1,0:T(8,128)}), f32[192,1152]{1,0:T(8,128)}) %all-reduce.2.cloned.1.call-update) | async-done | bytes 884752 | tf_op jit(solution)/shard_map/psum | solution.py:106
  139.1 1.5 multiply_reduce_fusion
  140.9 2.4 copy.22
  143.4 2.5 fusion.6
  145.9 1.9 fusion.74
  147.8 3.8 all-to-all-start.1
  151.6 11.3 %all-to-all-done.1 = f32[8,24,1152]{2,1,0:T(8,128)S(1)} async-done(((f32[8,24,1152]{2,1,0:T(8,128)}), f32[8,24,1152]{2,1,0:T(8,128)S(1)}, u32[]{:S(2)}, u32[]{:S(2)}) %all-to-all-start.1) | async-done | bytes 884768 | tf_op jit(solution)/shard_map/all_to_all | solution.py:44
  162.9 0.9 fusion.43
  163.9 0.9 fusion.45
  164.9 15.6 %all_to_all.41 = f32[8,24,1152]{2,1,0:T(8,128)S(1)} all-to-all(f32[8,24,1152]{2,1,0:T(8,128)S(1)} %broadcast_in_dim.36), channel_id=1, replica_groups=mesh['dp_0'=16,'dp_1'=2,'dp_2'=2,'mp'=8] {'mp'}, dimensions={0} | all-to-all | bytes 1769472 | tf_op jit(solution)/shard_map/all_to_all | solution.py:50
  180.5 4.1 fusion.28
  184.6 3.6 all-to-all-start.3
  188.3 12.4 %all-to-all-done.3 = f32[8,192,144]{1,2,0:T(8,128)S(1)} async-done(((f32[8,192,144]{1,2,0:T(8,128)}), f32[8,192,144]{1,2,0:T(8,128)S(1)}, u32[]{:S(2)}, u32[]{:S(2)}) %all-to-all-start.3) | async-done | bytes 884768 | tf_op jit(solution)/shard_map/all_to_all | solution.py:44
  201.4 1.0 copy.24
  203.3 4.0 all-to-all-start.4
  207.3 4.7 %convolution_convert_fusion = bf16[1536,1152]{1,0:T(8,128)(2,1)} fusion(bf16[192,1152]{1,0:T(8,128)(2,1)} %copy-done.5, f32[1536,192]{0,1:T(8,128)} %get-tuple-element.19, s32[1536]{0:T(1024)S(1)} %fusion.59, f32[]{:T(128)S(6)} %copy.32, s32[192]{0:T(256)S(1)} %iota_add_fusion), kind=kOutput, calls=%fused_computation | convolution fusion | flops 684195840 | bytes 5167876 | tf_op jit(solution)/shard_map/dot_general | solution.py:139
  212.0 2.9 all-to-all-done.4
  215.0 14.4 %all-to-all-start.5 = ((bf16[64,24,1152]{2,1,0:T(8,128)(2,1)}), bf16[64,24,1152]{2,1,0:T(8,128)(2,1)}, u32[]{:S(2)}, u32[]{:S(2)}) async-start(bf16[64,24,1152]{2,1,0:T(8,128)(2,1)} %bitcast.48), calls=%async_computation.5 | async-start | bytes 7077888 | tf_op jit(solution)/shard_map/all_to_all | solution.py:143
  229.4 162.7 %all-to-all-done.5 = bf16[64,24,1152]{2,1,0:T(8,128)(2,1)} async-done(((bf16[64,24,1152]{2,1,0:T(8,128)(2,1)}), bf16[64,24,1152]{2,1,0:T(8,128)(2,1)}, u32[]{:S(2)}, u32[]{:S(2)}) %all-to-all-start.5) | async-done | bytes 3538976 | tf_op jit(solution)/shard_map/all_to_all | solution.py:143
  392.1 2.5 convert_reduce_fusion
  394.9 0.8 broadcast_in_dim.40
  395.7 4.3 %all-to-all-start.6 = ((bf16[8,24,1152]{2,1,0:T(8,128)(2,1)}), bf16[8,24,1152]{2,1,0:T(8,128)(2,1)S(1)}, u32[]{:S(2)}, u32[]{:S(2)}) async-start(bf16[8,24,1152]{2,1,0:T(8,128)(2,1)} %broadcast_in_dim.40), calls=%async_computation.6 | async-start | bytes 884736 | tf_op jit(solution)/shard_map/all_to_all | solution.py:50
  400.0 1.2 multiply_add_fusion
  401.2 0.8 copy.26
  402.0 7.1 %all-to-all-done.6 = bf16[8,24,1152]{2,1,0:T(8,128)(2,1)S(1)} async-done(((bf16[8,24,1152]{2,1,0:T(8,128)(2,1)}), bf16[8,24,1152]{2,1,0:T(8,128)(2,1)S(1)}, u32[]{:S(2)}, u32[]{:S(2)}) %all-to-all-start.6) | async-done | bytes 442400 | tf_op jit(solution)/shard_map/all_to_all | solution.py:50
  409.1 1.0 fusion.75
  (47 shorter events, 3.6 us)
Async XLA Ops:
  8.0 25.7 %copy-start = (bf16[538,1152]{1,0:T(8,128)(2,1)S(1)}, bf16[538,1152]{1,0:T(8,128)(2,1)}, u32[]{:S(2)}) copy-start(bf16[538,1152]{1,0:T(8,128)(2,1)} %param.12) | copy-start | bytes 3718660
  8.0 96.7 %all-gather.3.cloned.1.call-start = ((), (), s32[]{:S(2)}) async-start(), calls=%async_computation.8 | async-start | bytes 1880064 | tf_op jit(solution)/shard_map/all_gather | solution.py:31
  9.5 21.7 %copy-start.1 = (bf16[192,1152]{1,0:T(8,128)(2,1)S(1)}, bf16[192,1152]{1,0:T(8,128)(2,1)}, u32[]{:S(2)}) copy-start(bf16[192,1152]{1,0:T(8,128)(2,1)} %param.8) | copy-start | bytes 1327108
  25.9 5.7 %copy-start.7 = (f32[1152]{0:T(1024)S(1)}, f32[1152]{0:T(1024)}, u32[]{:S(2)}) copy-start(f32[1152]{0:T(1024)} %param.10) | copy-start | bytes 13828
  31.2 107.9 %all-reduce.2.cloned.1.call-start = ((), (), s32[]{:S(2)}) async-start(), calls=%async_computation.7 | async-start | bytes 1769472 | tf_op jit(solution)/shard_map/psum | solution.py:106
  33.7 1.5 copy-start.6
  35.2 105.7 %all-gather.5.cloned.1.call-start = ((), (), s32[]{:S(2)}) async-start(), calls=%async_computation.9 | async-start | bytes 5308416 | tf_op jit(solution)/shard_map/all_gather | solution.py:31
  139.1 1.5 copy-start.2
  140.9 2.5 copy-start.5
  147.8 15.1 %all-to-all-start.1 = ((f32[8,24,1152]{2,1,0:T(8,128)}), f32[8,24,1152]{2,1,0:T(8,128)S(1)}, u32[]{:S(2)}, u32[]{:S(2)}) async-start(f32[8,24,1152]{2,1,0:T(8,128)} %fusion.74), calls=%async_computation.1 | async-start | bytes 1769472 | tf_op jit(solution)/shard_map/all_to_all | solution.py:44
  180.4 4.2 copy-start.4
  184.6 16.0 %all-to-all-start.3 = ((f32[8,192,144]{1,2,0:T(8,128)}), f32[8,192,144]{1,2,0:T(8,128)S(1)}, u32[]{:S(2)}, u32[]{:S(2)}) async-start(f32[8,192,144]{1,2,0:T(8,128)} %bitcast.53), calls=%async_computation.3 | async-start | bytes 2359296 | tf_op jit(solution)/shard_map/all_to_all | solution.py:44
  203.3 11.7 %all-to-all-start.4 = ((f32[8,1,384]{2,1,0:T(1,128)}), f32[8,1,384]{2,1,0:T(1,128)S(1)}, u32[]{:S(2)}, u32[]{:S(2)}) async-start(f32[8,1,384]{2,1,0:T(1,128)} %broadcast_in_dim.37), calls=%async_computation.4 | async-start | bytes 24576 | tf_op jit(solution)/shard_map/all_to_all | solution.py:50
  215.0 177.1 %all-to-all-start.5 = ((bf16[64,24,1152]{2,1,0:T(8,128)(2,1)}), bf16[64,24,1152]{2,1,0:T(8,128)(2,1)}, u32[]{:S(2)}, u32[]{:S(2)}) async-start(bf16[64,24,1152]{2,1,0:T(8,128)(2,1)} %bitcast.48), calls=%async_computation.5 | async-start | bytes 7077888 | tf_op jit(solution)/shard_map/all_to_all | solution.py:143
  394.9 14.2 %copy-start.3 = (bf16[144,1152]{1,0:T(8,128)(2,1)S(1)}, bf16[144,1152]{1,0:T(8,128)(2,1)}, u32[]{:S(2)}) copy-start(bf16[144,1152]{1,0:T(8,128)(2,1)} %param.13) | copy-start | bytes 995332
  395.7 13.4 %all-to-all-start.6 = ((bf16[8,24,1152]{2,1,0:T(8,128)(2,1)}), bf16[8,24,1152]{2,1,0:T(8,128)(2,1)S(1)}, u32[]{:S(2)}, u32[]{:S(2)}) async-start(bf16[8,24,1152]{2,1,0:T(8,128)(2,1)} %broadcast_in_dim.40), calls=%async_computation.6 | async-start | bytes 884736 | tf_op jit(solution)/shard_map/all_to_all | solution.py:50
Sparse Core Ops, SparseCore 0:
  31.3 73.3 all-gather.2
  106.8 20.0 all-gather.4
Sparse Core Ops, SparseCore 1:
  35.3 103.8 all-reduce.1
where the time goes:
time: 419 us; the launch traced here: 418 us
  waiting for transfers between devices  299 us (71%)
  blocking collectives  36.9 us (9%)
  starting transfers between devices  30.1 us (7%)
  matrix products  19.2 us (5%)
  between operations  17 us (4%)
  other arithmetic  9.52 us (2%)
  local copies, waits for them, and re-layouts  5.88 us (1%)
    all_to_all x1, waiting for transfers between devices, per_device(): lax.all_to_all(text_store.astype(jnp.bfloat16), DP, split_axis=0, concat_...  163 us
    all_gather x2, waiting for transfers between devices, stacked_from(): parts = lax.all_gather(parts, axes[k], axis=0, tiled=True)  69.5 us
    psum x1, waiting for transfers between devices, per_device(): image_out = image_float + lax.psum(partial_out, 'mp')  33 us
    all_to_all x2, waiting for transfers between devices, sum_at_owner(): lax.all_to_all(parts, axis, split_axis=0, concat_axis=0, tiled=True)  23.6 us
    all_to_all x1, blocking collectives, summed_on_arrival(): parts = lax.all_to_all(cut_along(array, dim, peers), axis, 0, 0, tiled=True)  16.4 us
    all_to_all x1, blocking collectives, sent_to_all(): return lax.all_to_all(copies, axis, split_axis=0, concat_axis=0, tiled=True)  15.6 us
    all_to_all x1, starting transfers between devices, per_device(): lax.all_to_all(text_store.astype(jnp.bfloat16), DP, split_axis=0, concat_...  14.4 us
    all_to_all x2, waiting for transfers between devices, sent_to_all(): return lax.all_to_all(copies, axis, split_axis=0, concat_axis=0, tiled=True)  10 us
  transfers between devices with their start and end apart: 8, of which 7 were waited for; matrix products, arithmetic and copies ran while one was open for 3% of the time, Pallas kernels for 0%

commit v1 on v0

--- a/solution.py
+++ b/solution.py
@@ -28,7 +28,8 @@
 def stacked_from(array, axes, order):
     parts = array[None]
     for k in order:
-        parts = lax.all_gather(parts, axes[k], axis=0, tiled=True)
+        outgoing = jnp.stack([parts] * lax.axis_size(axes[k]))
+        parts = jnp.concatenate(lax.all_to_all(outgoing, axes[k], 0, 0), axis=0)
     block = [lax.axis_size(axes[k]) for k in reversed(order)]
     parts = parts.reshape(*block, *array.shape)
     turned = sorted(range(len(order)), key=lambda place: order[len(order) - 1 - place])

time: 419 us -> 447 us (1.067)
  starting transfers between devices: 30.1 us -> 44.7 us
  blocking collectives: 36.9 us -> 48 us
    all_gather x2 -> x0, waiting for transfers between devices: 69.5 us -> none  [stacked_from(): parts = lax.all_gather(parts, axes[k], axis=0, tiled=True)]
    psum x1, waiting for transfers between devices: 33 us -> 100 us  [per_device(): image_out = image_float + lax.psum(partial_out, 'mp')]
    all_to_all x0 -> x1, starting transfers between devices: none -> 15 us  [stacked_from(): parts = jnp.concatenate(lax.all_to_all(outgoing, axes[k], 0, 0), axis=0)]
    all_to_all x0 -> x2, blocking collectives: none -> 12.9 us  [stacked_from(): parts = jnp.concatenate(lax.all_to_all(outgoing, axes[k], 0, 0), axis=0)]
    all_to_all x2, waiting for transfers between devices: 23.6 us -> 30.3 us  [sum_at_owner(): lax.all_to_all(parts, axis, split_axis=0, concat_axis=0, tiled=True)]
    all_gather x1 -> x0, blocking collectives: 4.93 us -> none  [stacked_from(): parts = lax.all_gather(parts, axes[k], axis=0, tiled=True)]
  transfers between devices with their start and end apart: 8 -> 7, of which waited for: 7 -> 6; matrix products, arithmetic and copies ran while one was open for 3% -> 3% of each run, Pallas kernels for 0% -> 0%
where the time goes in v1:
time: 447 us; the launch traced here: 446 us
  waiting for transfers between devices  303 us (68%)
  blocking collectives  48 us (11%)
  starting transfers between devices  44.7 us (10%)
  matrix products  18.7 us (4%)
  between operations  15.6 us (3%)
  other arithmetic  9.61 us (2%)
  local copies, waits for them, and re-layouts  6.22 us (1%)
    all_to_all x1, waiting for transfers between devices, per_device(): lax.all_to_all(text_store.astype(jnp.bfloat16), DP, split_axis=0, concat_...  163 us
    psum x1, waiting for transfers between devices, per_device(): image_out = image_float + lax.psum(partial_out, 'mp')  100 us
    all_to_all x2, waiting for transfers between devices, sum_at_owner(): lax.all_to_all(parts, axis, split_axis=0, concat_axis=0, tiled=True)  30.3 us
    all_to_all x1, blocking collectives, sent_to_all(): return lax.all_to_all(copies, axis, split_axis=0, concat_axis=0, tiled=True)  18.8 us
    all_to_all x1, blocking collectives, summed_on_arrival(): parts = lax.all_to_all(cut_along(array, dim, peers), axis, 0, 0, tiled=True)  16.3 us
    all_to_all x1, starting transfers between devices, stacked_from(): parts = jnp.concatenate(lax.all_to_all(outgoing, axes[k], 0, 0), axis=0)  15 us
    all_to_all x1, starting transfers between devices, per_device(): lax.all_to_all(text_store.astype(jnp.bfloat16), DP, split_axis=0, concat_...  14.8 us
    all_to_all x2, blocking collectives, stacked_from(): parts = jnp.concatenate(lax.all_to_all(outgoing, axes[k], 0, 0), axis=0)  12.9 us
  transfers between devices with their start and end apart: 7, of which 6 were waited for; matrix products, arithmetic and copies ran while one was open for 3% of the time, Pallas kernels for 0%

profile of v1, /device:TPU:8, one launch (start us, length us, event | category | flops | bytes accessed | tf_op | source)
XLA Modules:
  0.0 445.9 jit_solution(15980455903888004143)
XLA Ops:
  7.2 1.4 convolution_convert_fusion.1
  8.6 16.3 %all_to_all.55 = bf16[8,24,1152]{2,1,0:T(8,128)(2,1)S(1)} all-to-all(bf16[8,24,1152]{2,1,0:T(8,128)(2,1)S(1)} %bitcast.53), channel_id=1, replica_groups=mesh['dp_0'=16,'dp_1'=2,'dp_2'=2,'mp'=8] {'mp'}, dimensions={0} | all-to-all | bytes 884736 | tf_op jit(solution)/shard_map/all_to_all | solution.py:18
  25.7 6.4 %all_to_all.56 = bf16[2,1,24,1152]{3,2,1,0:T(8,128)(2,1)S(1)} all-to-all(bf16[2,1,24,1152]{3,2,1,0:T(8,128)(2,1)S(1)} %pad_maximum_fusion.1), channel_id=1, replica_groups=mesh['dp_0'=16,'dp_1'=2,'dp_2'=2,'mp'=8] {'dp_1'}, dimensions={0} | all-to-all | bytes 221184 | tf_op jit(solution)/shard_map/all_to_all | solution.py:32
  32.1 1.3 stack.10
  33.4 15.0 %all-to-all-start.2 = ((bf16[16,2,24,1152]{3,2,1,0:T(8,128)(2,1)}), bf16[16,2,24,1152]{3,2,1,0:T(8,128)(2,1)S(1)}, u32[]{:S(2)}, u32[]{:S(2)}) async-start(bf16[16,2,24,1152]{3,2,1,0:T(8,128)(2,1)} %stack.10), calls=%async_computation.2 | async-start | bytes 3538944 | tf_op jit(solution)/shard_map/all_to_all | solution.py:32
  49.0 2.0 fusion.22
  51.0 0.8 copy-done.7
  51.8 1.5 fusion.32
  54.6 100.1 %all-reduce.2.cloned.1.call-done = f32[192,1152]{1,0:T(8,128)} async-done(((f32[192,1152]{1,0:T(8,128)}), f32[192,1152]{1,0:T(8,128)}) %all-reduce.2.cloned.1.call-update) | async-done | bytes 884752 | tf_op jit(solution)/shard_map/psum | solution.py:107
  154.7 1.5 multiply_reduce_fusion
  156.2 1.4 fusion.7
  157.9 6.6 %all_to_all.57 = bf16[2,32,24,1152]{3,2,1,0:T(8,128)(2,1)S(1)} all-to-all(bf16[2,32,24,1152]{3,2,1,0:T(8,128)(2,1)S(1)} %pad_maximum_fusion), channel_id=1, replica_groups=mesh['dp_0'=16,'dp_1'=2,'dp_2'=2,'mp'=8] {'dp_2'}, dimensions={0} | all-to-all | bytes 7077888 | tf_op jit(solution)/shard_map/all_to_all | solution.py:32
  165.5 2.5 fusion.6
  168.0 1.9 fusion.74
  169.9 3.5 all-to-all-start.4
  173.5 14.7 %all-to-all-done.4 = f32[8,24,1152]{2,1,0:T(8,128)S(1)} async-done(((f32[8,24,1152]{2,1,0:T(8,128)}), f32[8,24,1152]{2,1,0:T(8,128)S(1)}, u32[]{:S(2)}, u32[]{:S(2)}) %all-to-all-start.4) | async-done | bytes 884768 | tf_op jit(solution)/shard_map/all_to_all | solution.py:45
  188.5 18.8 %all_to_all.58 = f32[8,24,1152]{2,1,0:T(8,128)S(1)} all-to-all(f32[8,24,1152]{2,1,0:T(8,128)S(1)} %broadcast_in_dim.35), channel_id=1, replica_groups=mesh['dp_0'=16,'dp_1'=2,'dp_2'=2,'mp'=8] {'mp'}, dimensions={0} | all-to-all | bytes 1769472 | tf_op jit(solution)/shard_map/all_to_all | solution.py:51
  207.3 3.7 fusion.28
  211.0 3.6 all-to-all-start.6
  214.7 15.6 %all-to-all-done.6 = f32[8,192,144]{1,2,0:T(8,128)S(1)} async-done(((f32[8,192,144]{1,2,0:T(8,128)}), f32[8,192,144]{1,2,0:T(8,128)S(1)}, u32[]{:S(2)}, u32[]{:S(2)}) %all-to-all-start.6) | async-done | bytes 884768 | tf_op jit(solution)/shard_map/all_to_all | solution.py:45
  230.5 1.2 multiply_reduce_fusion.2
  232.4 3.8 all-to-all-start.7
  236.2 4.8 %convolution_convert_fusion = bf16[1536,1152]{1,0:T(8,128)(2,1)} fusion(bf16[192,1152]{1,0:T(8,128)(2,1)} %get-tuple-element.15, f32[1536,192]{0,1:T(8,128)} %get-tuple-element.19, s32[1536]{0:T(1024)S(1)} %fusion.59, f32[]{:T(128)S(6)} %copy.31, s32[192]{0:T(256)S(1)} %iota_add_fusion), kind=kOutput, calls=%fused_computation | convolution fusion | flops 684195840 | bytes 5167876 | tf_op jit(solution)/shard_map/dot_general | solution.py:140
  241.0 2.9 all-to-all-done.7
  243.9 14.8 %all-to-all-start.8 = ((bf16[64,24,1152]{2,1,0:T(8,128)(2,1)}), bf16[64,24,1152]{2,1,0:T(8,128)(2,1)}, u32[]{:S(2)}, u32[]{:S(2)}) async-start(bf16[64,24,1152]{2,1,0:T(8,128)(2,1)} %bitcast.51), calls=%async_computation.8 | async-start | bytes 7077888 | tf_op jit(solution)/shard_map/all_to_all | solution.py:144
  258.7 162.7 %all-to-all-done.8 = bf16[64,24,1152]{2,1,0:T(8,128)(2,1)} async-done(((bf16[64,24,1152]{2,1,0:T(8,128)(2,1)}), bf16[64,24,1152]{2,1,0:T(8,128)(2,1)}, u32[]{:S(2)}, u32[]{:S(2)}) %all-to-all-start.8) | async-done | bytes 3538976 | tf_op jit(solution)/shard_map/all_to_all | solution.py:144
  421.4 2.5 convert_reduce_fusion
  424.2 0.8 broadcast_in_dim.39
  425.0 3.9 all-to-all-start.9
  429.0 1.2 multiply_add_fusion
  430.9 7.1 %all-to-all-done.9 = bf16[8,24,1152]{2,1,0:T(8,128)(2,1)S(1)} async-done(((bf16[8,24,1152]{2,1,0:T(8,128)(2,1)}), bf16[8,24,1152]{2,1,0:T(8,128)(2,1)S(1)}, u32[]{:S(2)}, u32[]{:S(2)}) %all-to-all-start.9) | async-done | bytes 442400 | tf_op jit(solution)/shard_map/all_to_all | solution.py:51
  438.1 1.0 fusion.75
  (51 shorter events, 5.2 us)
Async XLA Ops:
  7.2 44.6 %copy-start = (bf16[538,1152]{1,0:T(8,128)(2,1)S(1)}, bf16[538,1152]{1,0:T(8,128)(2,1)}, u32[]{:S(2)}) copy-start(bf16[538,1152]{1,0:T(8,128)(2,1)} %param.12) | copy-start | bytes 3718660
  25.0 0.6 copy-start.3
  33.4 15.1 %copy-start.1 = (bf16[192,1152]{1,0:T(8,128)(2,1)S(1)}, bf16[192,1152]{1,0:T(8,128)(2,1)}, u32[]{:S(2)}) copy-start(bf16[192,1152]{1,0:T(8,128)(2,1)} %param.8) | copy-start | bytes 1327108
  33.4 15.5 %copy-start.9 = (f32[1152]{0:T(1024)S(1)}, f32[1152]{0:T(1024)}, u32[]{:S(2)}) copy-start(f32[1152]{0:T(1024)} %param.10) | copy-start | bytes 13828
  33.4 124.1 %all-to-all-start.2 = ((bf16[16,2,24,1152]{3,2,1,0:T(8,128)(2,1)}), bf16[16,2,24,1152]{3,2,1,0:T(8,128)(2,1)S(1)}, u32[]{:S(2)}, u32[]{:S(2)}) async-start(bf16[16,2,24,1152]{3,2,1,0:T(8,128)(2,1)} %stack.10), calls=%async_computation.2 | async-start | bytes 3538944 | tf_op jit(solution)/shard_map/all_to_all | solution.py:32
  48.5 106.2 %all-reduce.2.cloned.1.call-start = ((), (), s32[]{:S(2)}) async-start(), calls=%async_computation.10 | async-start | bytes 1769472 | tf_op jit(solution)/shard_map/psum | solution.py:107
  51.0 0.8 copy-start.7
  154.7 1.5 copy-start.2
  164.5 1.0 copy-start.6
  169.9 18.3 %all-to-all-start.4 = ((f32[8,24,1152]{2,1,0:T(8,128)}), f32[8,24,1152]{2,1,0:T(8,128)S(1)}, u32[]{:S(2)}, u32[]{:S(2)}) async-start(f32[8,24,1152]{2,1,0:T(8,128)} %fusion.74), calls=%async_computation.4 | async-start | bytes 1769472 | tf_op jit(solution)/shard_map/all_to_all | solution.py:45
  188.5 18.9 %copy-start.8 = (f32[192,538]{1,0:T(8,128)S(1)}, f32[192,538]{1,0:T(8,128)}, u32[]{:S(2)}) copy-start(f32[192,538]{1,0:T(8,128)} %copy-done.7) | copy-start | bytes 1239556
  211.0 19.2 %all-to-all-start.6 = ((f32[8,192,144]{1,2,0:T(8,128)}), f32[8,192,144]{1,2,0:T(8,128)S(1)}, u32[]{:S(2)}, u32[]{:S(2)}) async-start(f32[8,192,144]{1,2,0:T(8,128)} %bitcast.56), calls=%async_computation.6 | async-start | bytes 2359296 | tf_op jit(solution)/shard_map/all_to_all | solution.py:45
  232.4 11.5 %all-to-all-start.7 = ((f32[8,1,384]{2,1,0:T(1,128)}), f32[8,1,384]{2,1,0:T(1,128)S(1)}, u32[]{:S(2)}, u32[]{:S(2)}) async-start(f32[8,1,384]{2,1,0:T(1,128)} %broadcast_in_dim.36), calls=%async_computation.7 | async-start | bytes 24576 | tf_op jit(solution)/shard_map/all_to_all | solution.py:51
  243.9 177.5 %all-to-all-start.8 = ((bf16[64,24,1152]{2,1,0:T(8,128)(2,1)}), bf16[64,24,1152]{2,1,0:T(8,128)(2,1)}, u32[]{:S(2)}, u32[]{:S(2)}) async-start(bf16[64,24,1152]{2,1,0:T(8,128)(2,1)} %bitcast.51), calls=%async_computation.8 | async-start | bytes 7077888 | tf_op jit(solution)/shard_map/all_to_all | solution.py:144
  258.7 165.2 %copy-start.4 = (f32[24,1152]{1,0:T(8,128)S(1)}, f32[24,1152]{1,0:T(8,128)}, u32[]{:S(2)}) copy-start(f32[24,1152]{1,0:T(8,128)} %copy-done.3) | copy-start | bytes 331780
  424.2 13.9 %copy-start.5 = (bf16[144,1152]{1,0:T(8,128)(2,1)S(1)}, bf16[144,1152]{1,0:T(8,128)(2,1)}, u32[]{:S(2)}) copy-start(bf16[144,1152]{1,0:T(8,128)(2,1)} %param.13) | copy-start | bytes 995332
  425.0 13.0 %all-to-all-start.9 = ((bf16[8,24,1152]{2,1,0:T(8,128)(2,1)}), bf16[8,24,1152]{2,1,0:T(8,128)(2,1)S(1)}, u32[]{:S(2)}, u32[]{:S(2)}) async-start(bf16[8,24,1152]{2,1,0:T(8,128)(2,1)} %broadcast_in_dim.39), calls=%async_computation.9 | async-start | bytes 884736 | tf_op jit(solution)/shard_map/all_to_all | solution.py:51
Sparse Core Ops, SparseCore 0:
  53.4 101.2 all-reduce.1
